TPU v7x, 256 devices: a whole 4x4x8 slice. The times are simulated.
256 devices in a mesh: img: 4 (over x), seq: 8 (over z_lo, y), tp: 8 (over z_hi, core).
Axes of the slice: x: 4, y: 4, z: 8 (z_hi: 4, z_lo: 2; z = z_hi * 2 + z_lo), core: 2. Of those that a mesh axis runs over, the one named last changes fastest.
Arguments:
- vit_qkv: bfloat16 [4, 4096, 3, 1280], P('img', ('seq', 'tp')), may hold values from -6 to 6
- patch_counts: int32 [4], P('img'), may hold values from 1024 to 4096, as said below
- vit_out_weight: bfloat16 [1280, 1280], replicated, may hold values from -0.15625 to 0.15625
- vit_norm_gain: float32 [1280], replicated, may hold values from 0.25 to 1.75
- merger_weight: bfloat16 [5120, 8192], P(('img', 'seq'), 'tp'), may hold values from -8 to 8
- lm_norm_gain: float32 [8192], P('tp'), may hold values from 0.25 to 1.75
- kv_weight: bfloat16 [8192, 2048], P('tp', ('img', 'seq')), may hold values from -0.0625 to 0.0625
- queries: bfloat16 [4, 4096, 64, 128], P('img', 'seq', 'tp'), may hold values from -6 to 6
- span_kv: bfloat16 [4, 4096, 2, 8, 128], P('img', 'seq', None, 'tp'), may hold values from -6 to 6
Outputs:
- lm_attention: bfloat16 [4, 4096, 64, 128], P('img', 'seq', 'tp')
Inputs may be any that keep to these rules, and one draw needn't show every extreme that they name: `patch_counts`: each count is a multiple of 4, at least 1024, and some image has exactly 4096.
All inputs are finite; a program needn't handle non-finite values.
Results may differ from a plain program's by a relative error of at most 0.04.
Values may be sent and summed in bfloat16 or wider, within the bound.
A program may use at most 128 MiB of HBM per device.

v0:
```python
import jax
import jax.numpy as jnp
from jax import lax
from jax.sharding import Mesh
from jax.sharding import PartitionSpec as P

VIT_D = 1280
VIT_HEADS = 16
VIT_HDIM = 80
D = 8192
HQ = 64
KVH = 8
HD = 128
SEQ = ("seq_0", "seq_1")
IMG_SEQ = ("img", "seq_0", "seq_1")
SEQ_TP = ("seq_0", "seq_1", "tp")
masked_score = -1e30


def sent_to_all(x, axis):
    copies = jnp.broadcast_to(x, (lax.axis_size(axis), *x.shape))
    return lax.all_to_all(copies, axis, split_axis=0, concat_axis=0, tiled=True)


def in_order(parts, dim):
    parts = jnp.moveaxis(parts, 0, dim)
    lengths = parts.shape
    return parts.reshape(*lengths[:dim], lengths[dim] * lengths[dim + 1], *lengths[dim + 2 :])


def gather_directly(x, axis, dim):
    parts = sent_to_all(x, axis)
    return in_order(parts, dim)


def in_one_piece(arrays, axis, dim, along):
    ends, at = ([], 0)
    for a in arrays[:-1]:
        at += a.shape[along]
        ends.append(at)
    both = jnp.concatenate(arrays, axis=along)
    return tuple(jnp.split(gather_directly(both, axis, dim), ends, axis=along))


def all_blocks(x, axes, sequence):
    parts = x[None]
    for k in sequence:
        parts = lax.all_gather(parts, axes[k], axis=0, tiled=True)
    current = [lax.axis_size(axes[k]) for k in reversed(sequence)]
    parts = parts.reshape(*current, *x.shape)
    turned = sorted(range(len(sequence)), key=lambda place: sequence[len(sequence) - 1 - place])
    return parts.transpose(*turned, *range(len(sequence), parts.ndim)).reshape(-1, *x.shape)


def gathered_by_axis(x, axes, sequence, dim):
    return in_order(all_blocks(x, axes, sequence), dim)


def over_copies(x, axis):
    return sent_to_all(x, axis).sum(axis=0)


def in_blocks(x, dim, length):
    before, after = (x.shape[:dim], x.shape[dim + 1 :])
    return jnp.moveaxis(x.reshape(*before, length, -1, *after), dim, 0)


def sum_at_owner(x, axis, dim):
    length = lax.axis_size(axis)
    parts = lax.all_to_all(in_blocks(x, dim, length), axis, 0, 0, tiled=True)
    return jnp.sum(parts.astype(jnp.float32), axis=0)


def in_one_piece_2(arrays, axis, dim, along):
    widths = [a.shape[along] for a in arrays]
    both = jnp.concatenate(arrays, axis=along)
    out = lax.all_gather(both, axis, axis=dim, tiled=True)
    return tuple(jnp.split(out, [sum(widths[:k]) for k in range(1, len(widths))], axis=along))


def fold_block(running, scores, usable, value_block, forms):
    peak, weight_sum, blended = running
    scores = jnp.where(usable, scores, masked_score)
    new_peak = jnp.maximum(peak, jnp.max(scores, axis=-1))
    weights = jnp.where(usable, jnp.exp(scores - new_peak[..., None]), 0.0)
    decay = jnp.exp(peak - new_peak)
    weight_sum = weight_sum * decay + jnp.sum(weights, axis=-1)
    blended = blended * decay[..., None] + jnp.einsum(
        forms, weights.astype(jnp.bfloat16), value_block, preferred_element_type=jnp.float32
    )
    return (new_peak, weight_sum, blended)


def local(
    vit_qkv,
    patch_counts,
    vit_out_weight,
    vit_norm_gain,
    merger_weight,
    lm_norm_gain,
    kv_weight,
    queries,
    span_kv,
):
    patch_rows = vit_qkv.shape[1]
    tp_count = lax.axis_size("tp")
    seq_index = lax.axis_index(SEQ)
    tp_index = lax.axis_index("tp")
    patch_total = patch_counts[0]
    local_qkv = vit_qkv[0].reshape(patch_rows, 3, VIT_HEADS, VIT_HDIM)
    scaling = VIT_HDIM ** (-0.5)
    spread = lax.all_to_all(local_qkv, SEQ, split_axis=2, concat_axis=0, tiled=True)
    local_rows = spread.shape[0]

    def seq_rows(index):
        source = index // local_rows
        within = index % local_rows
        return (within // patch_rows * tp_count + source) * patch_rows + within % patch_rows

    heads_local = spread.shape[2]
    query_count = spread.shape[0]
    query_rows = spread[:, 0]
    running = (
        jnp.full((heads_local, query_count), masked_score, jnp.float32),
        jnp.zeros((heads_local, query_count), jnp.float32),
        jnp.zeros((heads_local, query_count, VIT_HDIM), jnp.float32),
    )
    make_heads_local = query_rows.shape[1]
    key_piece, value_piece = in_one_piece((spread[:, 1], spread[:, 2]), "tp", 0, 1)
    blocks = key_piece.shape[0] // local_rows
    key_blocks = key_piece.reshape(blocks, local_rows, make_heads_local, VIT_HDIM)
    value_blocks = value_piece.reshape(blocks, local_rows, make_heads_local, VIT_HDIM)
    offsets = jnp.arange(blocks, dtype=jnp.int32) * local_rows

    def make_advance(state, inputs):
        key_block, value_block, offset = inputs
        usable = seq_rows(offset + jnp.arange(local_rows, dtype=jnp.int32)) < patch_total
        scores = (
            jnp.einsum("qhd,khd->hqk", query_rows, key_block, preferred_element_type=jnp.float32)
            * scaling
        )
        return (fold_block(state, scores, usable[None, None, :], value_block, "hqk,khd->hqd"), None)

    result, _ = lax.scan(make_advance, running, (key_blocks, value_blocks, offsets))
    state = result
    peak, weight_sum, blended = state
    returned = lax.all_to_all(
        jnp.transpose(blended / weight_sum[..., None], (1, 0, 2)).astype(jnp.bfloat16),
        SEQ,
        split_axis=0,
        concat_axis=1,
        tiled=True,
    )
    attended = returned.reshape(patch_rows, VIT_D)
    hidden = jnp.dot(attended, vit_out_weight, preferred_element_type=jnp.float32)
    patch_ids = (seq_index * tp_count + tp_index) * patch_rows + jnp.arange(
        patch_rows, dtype=jnp.int32
    )
    hidden = jnp.where((patch_ids < patch_total)[:, None], hidden, 0.0)
    centred = hidden - jnp.mean(hidden, axis=-1, keepdims=True)
    spread_sq = jnp.mean(centred * centred, axis=-1, keepdims=True)
    normed = (centred * lax.rsqrt(spread_sq + 1e-06) * vit_norm_gain).astype(jnp.bfloat16)
    merged_local = normed.reshape(patch_rows // 4, 4 * VIT_D)
    token_rows = gather_directly(merged_local, "tp", 0)
    embedded_sum = jnp.dot(
        token_rows,
        gathered_by_axis(merger_weight, IMG_SEQ, (1, 0, 2), 0),
        preferred_element_type=jnp.float32,
    )
    embedded = lax.optimization_barrier(embedded_sum.astype(jnp.bfloat16))
    embedded_wide = embedded.astype(jnp.float32)
    square_sums = over_copies(jnp.sum(embedded_wide * embedded_wide, axis=-1), "tp")
    lm_normed = (embedded_wide * lax.rsqrt(square_sums[:, None] / D + 1e-06) * lm_norm_gain).astype(
        jnp.bfloat16
    )
    kv_terms = jnp.dot(
        lm_normed,
        lax.all_gather(kv_weight, IMG_SEQ, axis=1, tiled=True),
        preferred_element_type=jnp.float32,
    )
    visual_count = kv_terms.shape[0]
    kv_terms = kv_terms.reshape(visual_count, 2, KVH, HD)
    visual_kv = sum_at_owner(kv_terms.astype(jnp.bfloat16), "tp", 2).astype(jnp.bfloat16)
    span_rows = queries.shape[1]
    kv_local = span_kv.shape[3]
    groups = HQ // KVH
    lm_scaling = HD ** (-0.5)
    grouped = queries[0].reshape(span_rows, kv_local, groups, HD)
    causal = jnp.arange(span_rows)[:, None] >= jnp.arange(span_rows)[None, :]
    near_scores = (
        jnp.einsum("ckgd,nkd->kgcn", grouped, span_kv[0, :, 0], preferred_element_type=jnp.float32)
        * lm_scaling
    )
    initial = (
        jnp.full((kv_local, groups, span_rows), masked_score, jnp.float32),
        jnp.zeros((kv_local, groups, span_rows), jnp.float32),
        jnp.zeros((kv_local, groups, span_rows, HD), jnp.float32),
    )
    initial = fold_block(
        initial, near_scores, causal[None, None], span_kv[0, :, 1], "kgcn,nkd->kgcd"
    )
    visual_total = patch_total // 4
    key_piece, value_piece = in_one_piece_2((visual_kv[:, 0], visual_kv[:, 1]), SEQ, 0, 1)
    blocks = key_piece.shape[0] // visual_count
    key_blocks = key_piece.reshape(blocks, visual_count, kv_local, HD)
    value_blocks = value_piece.reshape(blocks, visual_count, kv_local, HD)
    offsets = jnp.arange(blocks, dtype=jnp.int32) * visual_count

    def visual_advance(state, inputs):
        key_block, value_block, offset = inputs
        usable = offset + jnp.arange(visual_count, dtype=jnp.int32) < visual_total
        scores = (
            jnp.einsum("ckgd,nkd->kgcn", grouped, key_block, preferred_element_type=jnp.float32)
            * lm_scaling
        )
        return (
            fold_block(state, scores, usable[None, None, None, :], value_block, "kgcn,nkd->kgcd"),
            None,
        )

    result, _ = lax.scan(visual_advance, initial, (key_blocks, value_blocks, offsets))
    peak, weight_sum, blended = result
    result = jnp.transpose(blended / weight_sum[..., None], (2, 0, 1, 3))
    return result.reshape(span_rows, kv_local * groups, HD).astype(jnp.bfloat16)[None]


def solution(mesh):
    torus = Mesh(
        mesh.devices.reshape(mesh.shape["img"], 2, 4, mesh.shape["tp"]),
        ("img", "seq_0", "seq_1", "tp"),
    )
    placed = (
        P("img", SEQ_TP, None, None),
        P("img"),
        P(),
        P(),
        P(IMG_SEQ, "tp"),
        P("tp"),
        P("tp", IMG_SEQ),
        P("img", SEQ, "tp", None),
        P("img", SEQ, None, "tp", None),
    )
    return jax.shard_map(
        local, mesh=torus, in_specs=placed, out_specs=P("img", SEQ, "tp", None), check_vma=False
    )
```

profile of v0, /device:TPU:14, one launch (start us, length us, event | category | flops | bytes accessed | tf_op | source)
XLA Modules:
  0.0 454.1 jit_solution(11617065756509815237)
XLA Ops:
  6.5 12.6 %all-gather = bf16[320,1024]{1,0:T(8,128)(2,1)} all-gather(bf16[160,1024]{1,0:T(8,128)(2,1)} %param.17), channel_id=2, replica_groups=mesh['img'=4,'seq_0'=2,'seq_1'=4,'tp'=8] {'seq_0'}, dimensions={0}, use_global_device_ids=true | all-gather | bytes 983040 | tf_op jit(solution)/shard_map/all_gather | solution.py:48
  19.2 37.9 %all-gather.5.cloned.1.call-done = bf16[8,160,1024]{2,1,0:T(8,128)(2,1)} async-done(((bf16[2,160,1024]{2,1,0:T(8,128)(2,1)}), bf16[8,160,1024]{2,1,0:T(8,128)(2,1)}) %all-gather.5.cloned.1.call-update) | async-done | bytes 2621456 | tf_op jit(solution)/shard_map/all_gather | solution.py:48
  61.3 16.7 %all_to_all.54 = bf16[64,3,16,80]{3,0,1,2:T(8,128)(2,1)} all-to-all(bf16[64,3,16,80]{3,0,1,2:T(8,128)(2,1)S(1)} %copy.154), channel_id=1, replica_groups=mesh['img'=4,'seq_0'=2,'seq_1'=4,'tp'=8] {'seq_0','seq_1'}, dimensions={2} | all-to-all | bytes 983040 | tf_op jit(solution)/shard_map/all_to_all | solution.py:112
  85.8 6.1 %all-to-all-start.1 = ((bf16[8,512,4,80]{1,3,2,0:T(8,128)(2,1)}), bf16[8,512,4,80]{1,3,2,0:T(8,128)(2,1)}, u32[]{:S(2)}, u32[]{:S(2)}) async-start(bf16[8,512,4,80]{1,3,2,0:T(8,128)(2,1)} %broadcast_in_dim.148), calls=%async_computation.1 | async-start | bytes 5242880 | tf_op jit(solution)/shard_map/all_to_all | solution.py:22
  92.6 62.4 %all-to-all-done.1 = bf16[8,512,4,80]{1,3,2,0:T(8,128)(2,1)} async-done(((bf16[8,512,4,80]{1,3,2,0:T(8,128)(2,1)}), bf16[8,512,4,80]{1,3,2,0:T(8,128)(2,1)}, u32[]{:S(2)}, u32[]{:S(2)}) %all-to-all-start.1) | async-done | bytes 2621472 | tf_op jit(solution)/shard_map/all_to_all | solution.py:22
  159.1 76.2 %while.33 = (s32[]{:T(128)}, f32[2,512]{1,0:T(2,128)S(1)}, f32[2,512]{1,0:T(2,128)S(1)}, f32[2,512,80]{1,2,0:T(8,128)}, s32[8]{0:T(128)S(1)}, /*index=5*/s32[]{:...) while((s32[]{:T(128)}, f32[2,512]{1,0:T(2,128)S(1)}, ...), condition=%wide.region_5.6_spmd.clone, body=%wide.region_2.5_spmd.clone.sunk | while | flops 174861312 | bytes 15896233 | solution.py:144
  237.2 4.3 all-to-all-start.2
  242.2 6.0 %all-to-all-done.2 = bf16[512,2,80]{2,1,0:T(2,128)(2,1)S(1)} async-done(((bf16[512,2,80]{2,1,0:T(2,128)(2,1)}), bf16[512,2,80]{2,1,0:T(2,128)(2,1)S(1)}, u32[]{:S(2)}, u32[]{:S(2)}) %all-to-all-start.2) | async-done | bytes 163872 | tf_op jit(solution)/shard_map/all_to_all | solution.py:147
  254.8 3.9 all-to-all-start.3
  259.8 4.9 %fusion.55 = (f32[8,512]{1,0:T(8,128)S(1)}, f32[512,512,8]{1,0,2:T(8,128)}) fusion(pred[512,512]{0,1:T(8,128)(4,1)S(1)} %iota_compare_fusion, bf16[512,8,128]{2,1,0:T(8,128)(2,1)S(1)} %bitcast.250, bf16[1,512,1,1,128]{4,2,3,1,0:T(2,128)(2,1)S(1)} %get-tuple-element.403), kind=kOutput, calls=%fused_computation.84 | convolution fusion | flops 543158272 | bytes 9846784 | tf_op jit(solution)/shard_map/ckgd,nkd->kgcn/dot_general | solution.py:191
  264.8 9.9 %copy.165 = bf16[4,2,4,160,1024]{4,3,2,1,0:T(8,128)(2,1)} copy(bf16[4,2,4,160,1024]{4,3,1,0,2:T(8,128)(2,1)} %bitcast.243) | data formatting | bytes 20971520 | tf_op jit(solution)/shard_map/transpose | solution.py:52
  274.7 18.9 %all-to-all-done.3 = bf16[8,16,5120]{2,1,0:T(8,128)(2,1)S(1)} async-done(((bf16[8,16,5120]{2,1,0:T(8,128)(2,1)}), bf16[8,16,5120]{2,1,0:T(8,128)(2,1)S(1)}, u32[]{:S(2)}, u32[]{:S(2)}) %all-to-all-start.3) | async-done | bytes 1310752 | tf_op jit(solution)/shard_map/all_to_all | solution.py:22
  293.6 5.5 %convolution_convert_fusion.1 = bf16[128,1024]{1,0:T(8,128)(2,1)S(1)} fusion(bf16[128,5120]{1,0:T(8,128)(2,1)S(1)} %bitcast.247, bf16[5120,1024]{1,0:T(8,128)(2,1)} %bitcast.241), kind=kOutput, calls=%fused_computation.98 | convolution fusion | flops 1342308352 | bytes 12058624 | tf_op jit(solution)/shard_map/dot_general | solution.py:165
  299.9 3.3 all-to-all-start.4
  303.2 4.5 fusion.57
  307.7 3.0 all-to-all-done.4
  310.8 17.5 %all-gather.9.cloned.1.call-done = bf16[1024,2048]{0,1:T(8,128)(2,1)} async-done(((bf16[1024,64]{0,1:T(8,128)(2,1)}), bf16[1024,2048]{0,1:T(8,128)(2,1)}) %all-gather.9.cloned.1.call-update) | async-done | bytes 4194320 | tf_op jit(solution)/shard_map/all_gather | solution.py:178
  328.3 3.7 fusion.65
  333.3 5.1 %all-to-all-start.5 = ((bf16[8,128,2,1,128]{4,2,1,3,0:T(2,128)(2,1)}), bf16[8,128,2,1,128]{4,2,1,3,0:T(2,128)(2,1)}, u32[]{:S(2)}, u32[]{:S(2)}) async-start(bf16[8,128,2,1,128]{4,2,1,3,0:T(2,128)(2,1)} %bitcast.189), calls=%async_computation.5 | async-start | bytes 1048576 | tf_op jit(solution)/shard_map/all_to_all | solution.py:70
  338.6 7.4 %add_bitcast_fusion = f32[1,8,512,128]{3,2,1,0:T(8,128)} fusion(f32[512,512,8]{1,0,2:T(8,128)} %get-tuple-element.412, f32[8,512]{1,0:T(8,128)S(1)} %get-tuple-element.408, pred[512,512]{0,1:T(8,128)(4,1)S(1)} %iota_compare_fusion, f32[8,512]{1,0:T(8,128)S(1)} %get-tuple-element.406, bf16[1,512,1,1,128]{4,2,3,1,0:T(2,128)(2,1)S(1)} %copy-done.7), kind=kOutput, calls=%fused_computation.94 | convolution fusion | flops 547880960 | bytes 10911744 | tf_op jit(solution)/shard_map/kgcn,nkd->kgcd/dot_general | solution.py:88
  346.0 10.9 %all-to-all-done.5 = bf16[8,128,2,1,128]{4,2,1,3,0:T(2,128)(2,1)} async-done(((bf16[8,128,2,1,128]{4,2,1,3,0:T(2,128)(2,1)}), bf16[8,128,2,1,128]{4,2,1,3,0:T(2,128)(2,1)}, u32[]{:S(2)}, u32[]{:S(2)}) %all-to-all-start.5) | async-done | bytes 524320 | tf_op jit(solution)/shard_map/all_to_all | solution.py:70
  358.6 34.6 %all_gather.19 = bf16[1024,2,128]{2,0,1:T(8,128)(2,1)S(1)} all-gather(bf16[128,2,128]{2,0,1:T(8,128)(2,1)S(1)} %pad_maximum_fusion.1), channel_id=1, replica_groups=mesh['img'=4,'seq_0'=2,'seq_1'=4,'tp'=8] {'seq_0','seq_1'}, dimensions={0}, use_global_device_ids=true | all-gather | bytes 589824 | tf_op jit(solution)/shard_map/all_gather | solution.py:77
  393.9 49.6 %while.32 = (s32[]{:T(128)}, f32[1,8,512]{2,1,0:T(8,128)S(1)}, f32[1,8,512]{2,1,0:T(8,128)S(1)}, f32[1,8,512,128]{3,2,1,0:T(8,128)}, s32[8]{0:T(128)S(1)}, /*ind...) while((s32[]{:T(128)}, f32[1,8,512]{2,1,0:T(8,128)S(1)}, ...), condition=%wide.region_14.15_spmd, body=%wide.region_11.14_spmd.sunk | while | flops 276312320 | bytes 28641840 | solution.py:221
  443.7 3.9 fusion.68
  (243 shorter events, 156.3 us)
Async XLA Ops:
  6.5 244.8 %copy-start = (bf16[1280,1280]{1,0:T(8,128)(2,1)S(1)}, bf16[1280,1280]{1,0:T(8,128)(2,1)}, u32[]{:S(2)}) copy-start(bf16[1280,1280]{1,0:T(8,128)(2,1)} %param.15) | copy-start | bytes 9830404
  6.5 50.6 %all-gather.5.cloned.1.call-start = ((), (), s32[]{:S(2)}) async-start(), calls=%async_computation.6 | async-start | bytes 3276800 | tf_op jit(solution)/shard_map/all_gather | solution.py:48
  19.1 245.6 %all-gather.7.cloned.1.call-start = ((), (), s32[]{:S(2)}) async-start(), calls=%async_computation.7 | async-start | bytes 13107200 | tf_op jit(solution)/shard_map/all_gather | solution.py:48
  85.8 69.3 %all-to-all-start.1 = ((bf16[8,512,4,80]{1,3,2,0:T(8,128)(2,1)}), bf16[8,512,4,80]{1,3,2,0:T(8,128)(2,1)}, u32[]{:S(2)}, u32[]{:S(2)}) async-start(bf16[8,512,4,80]{1,3,2,0:T(8,128)(2,1)} %broadcast_in_dim.148), calls=%async_computation.1 | async-start | bytes 5242880 | tf_op jit(solution)/shard_map/all_to_all | solution.py:22
  91.9 236.4 %all-gather.9.cloned.1.call-start = ((), (), s32[]{:S(2)}) async-start(), calls=%async_computation.8 | async-start | bytes 4325376 | tf_op jit(solution)/shard_map/all_gather | solution.py:178
  192.2 2.4 copy-start.2
  230.4 2.4 copy-start.2
  237.2 10.9 %all-to-all-start.2 = ((bf16[512,2,80]{2,1,0:T(2,128)(2,1)}), bf16[512,2,80]{2,1,0:T(2,128)(2,1)S(1)}, u32[]{:S(2)}, u32[]{:S(2)}) async-start(bf16[512,2,80]{2,1,0:T(2,128)(2,1)} %bitcast.256), calls=%async_computation.2 | async-start | bytes 524288 | tf_op jit(solution)/shard_map/all_to_all | solution.py:147
  253.5 5.2 %copy-start.6 = (bf16[1,512,2,1,128]{4,2,3,1,0:T(2,128)(2,1)S(1)}, bf16[1,512,2,1,128]{4,2,3,1,0:T(2,128)(2,1)}, u32[]{:S(2)}) copy-start(bf16[1,512,2,1,128]{4,2,3,1,0:T(2,128)(2,1)} %param.21) | copy-start | bytes 786436
  254.8 5.1 %copy-start.5 = (bf16[1,512,8,128]{3,2,1,0:T(8,128)(2,1)S(1)}, bf16[1,512,8,128]{3,2,1,0:T(8,128)(2,1)}, u32[]{:S(2)}) copy-start(bf16[1,512,8,128]{3,2,1,0:T(8,128)(2,1)} %param.20) | copy-start | bytes 3145732
  254.8 38.8 %all-to-all-start.3 = ((bf16[8,16,5120]{2,1,0:T(8,128)(2,1)}), bf16[8,16,5120]{2,1,0:T(8,128)(2,1)S(1)}, u32[]{:S(2)}, u32[]{:S(2)}) async-start(bf16[8,16,5120]{2,1,0:T(8,128)(2,1)} %broadcast_in_dim.150), calls=%async_computation.3 | async-start | bytes 2621440 | tf_op jit(solution)/shard_map/all_to_all | solution.py:22
  299.9 10.9 %all-to-all-start.4 = ((f32[8,1,128]{2,1,0:T(1,128)}), f32[8,1,128]{2,1,0:T(1,128)S(1)}, u32[]{:S(2)}, u32[]{:S(2)}) async-start(f32[8,1,128]{2,1,0:T(1,128)} %broadcast_in_dim.152), calls=%async_computation.4 | async-start | bytes 8192 | tf_op jit(solution)/shard_map/all_to_all | solution.py:22
  303.2 25.1 %copy-start.9 = (f32[1024]{0:T(1024)S(1)}, f32[1024]{0:T(1024)}, u32[]{:S(2)}) copy-start(f32[1024]{0:T(1024)} %param.18) | copy-start | bytes 12292
  332.1 6.5 %copy-start.7 = (bf16[1,512,1,1,128]{4,2,3,1,0:T(2,128)(2,1)S(1)}, bf16[1,512,1,1,128]{4,2,3,1,0:T(2,128)(2,1)}, u32[]{:S(2)}) copy-start(bf16[1,512,1,1,128]{4,2,3,1,0:T(2,128)(2,1)} %get-tuple-element.402) | copy-start | bytes 393220
  333.3 23.6 %all-to-all-start.5 = ((bf16[8,128,2,1,128]{4,2,1,3,0:T(2,128)(2,1)}), bf16[8,128,2,1,128]{4,2,1,3,0:T(2,128)(2,1)}, u32[]{:S(2)}, u32[]{:S(2)}) async-start(bf16[8,128,2,1,128]{4,2,1,3,0:T(2,128)(2,1)} %bitcast.189), calls=%async_computation.5 | async-start | bytes 1048576 | tf_op jit(solution)/shard_map/all_to_all | solution.py:70
  393.9 2.5 copy-start.3
  400.1 2.6 copy-start.3
  406.3 2.6 copy-start.3
  412.5 2.6 copy-start.3
  418.7 2.6 copy-start.3
  424.9 2.6 copy-start.3
  431.1 2.6 copy-start.3
  437.3 2.6 copy-start.3
  443.5 4.0 copy-start.1
  (15 other events, 26.8 us)
Sparse Core Ops, SparseCore 0:
  19.3 37.7 all-gather.4
  58.9 105.2 all-gather.6
  166.0 162.2 all-gather.8
where the time goes:
time: 457 us; the launch traced here: 454 us
  waiting for transfers between devices  157 us (34%)
  matrix products  92.9 us (20%)
  blocking collectives  63.8 us (14%)
  local copies, waits for them, and re-layouts  51.3 us (11%)
  other arithmetic  51.2 us (11%)
  starting transfers between devices  22.7 us (5%)
  between operations  14.1 us (3%)
    all_to_all x3, waiting for transfers between devices, sent_to_all(): return lax.all_to_all(copies, axis, split_axis=0, concat_axis=0, tiled=True)  84.3 us
    dot_general x17, matrix products, fold_block(): jnp.einsum(forms, weights.astype(jnp.bfloat16), value_block, preferred_el...  45.3 us
    all_gather x2, waiting for transfers between devices, all_blocks(): parts = lax.all_gather(parts, axes[k], axis=0, tiled=True)  37.9 us
    all_gather x1, blocking collectives, in_one_piece_2(): out = lax.all_gather(both, axis, axis=dim, tiled=True)  34.6 us
    reduce_sum x17, other arithmetic, fold_block(): weight_sum = weight_sum * decay + jnp.sum(weights, axis=-1)  28.1 us
    dot_general x8, matrix products, make_advance(): jnp.einsum('qhd,khd->hqk', query_rows, key_block, preferred_element_type=...  22 us
    all_gather x1, waiting for transfers between devices, local(): lax.all_gather(kv_weight, IMG_SEQ, axis=1, tiled=True)  17.5 us
    all_to_all x1, blocking collectives, local(): lax.all_to_all(local_qkv, SEQ, split_axis=2, concat_axis=0, tiled=True)  16.7 us
  transfers between devices with their start and end apart: 8, of which 7 were waited for; matrix products, arithmetic and copies ran while one was open for 29% of the time, Pallas kernels for 0%

commit v1 on v0

--- a/solution.py
+++ b/solution.py
@@ -45,7 +45,10 @@
 def all_blocks(x, axes, sequence):
     parts = x[None]
     for k in sequence:
-        parts = lax.all_gather(parts, axes[k], axis=0, tiled=True)
+        size = lax.axis_size(axes[k])
+        pieces = jnp.stack([parts for _ in range(size)])
+        pieces = lax.all_to_all(pieces, axes[k], split_axis=0, concat_axis=0)
+        parts = jnp.concatenate(pieces, axis=0)
     current = [lax.axis_size(axes[k]) for k in reversed(sequence)]
     parts = parts.reshape(*current, *x.shape)
     turned = sorted(range(len(sequence)), key=lambda place: sequence[len(sequence) - 1 - place])

time: 457 us -> 579 us (1.27)
  waiting for transfers between devices: 157 us -> 252 us
  blocking collectives: 63.8 us -> 40.7 us
  starting transfers between devices: 22.7 us -> 45.3 us
  local copies, waits for them, and re-layouts: 51.3 us -> 70.3 us
  other arithmetic: 51.2 us -> 64.2 us
    all_to_all x1 -> x4, waiting for transfers between devices: 5.97 us -> 158 us  [the longest x3 149 us: all_blocks(): pieces = lax.all_to_all(pieces, axes[k], split_axis=0, concat_axis=0)]
    all_gather x2 -> x0, waiting for transfers between devices: 37.9 us -> none  [all_blocks(): parts = lax.all_gather(parts, axes[k], axis=0, tiled=True)]
    all_to_all x1 -> x4, starting transfers between devices: 4.28 us -> 23.3 us  [the longest x3 17 us: all_blocks(): pieces = lax.all_to_all(pieces, axes[k], split_axis=0, concat_axis=0)]
    all_gather x1, waiting for transfers between devices: 17.5 us -> 0.01 us  [local(): lax.all_gather(kv_weight, IMG_SEQ, axis=1, tiled=True)]
    all_gather x1 -> x0, blocking collectives: 12.6 us -> none  [all_blocks(): parts = lax.all_gather(parts, axes[k], axis=0, tiled=True)]
    add x17, other arithmetic: 0.26 us -> 11.4 us  [fold_block(): weight_sum = weight_sum * decay + jnp.sum(weights, axis=-1)]
    another operation x0 -> x2, local copies, waits for them, and re-layouts: none -> 10 us  [all_blocks(): pieces = jnp.stack([parts for _ in range(size)])]
    transpose x1 -> x0, local copies, waits for them, and re-layouts: 9.88 us -> none  [all_blocks(): parts.transpose(*turned, *range(len(sequence), parts.ndim))]
  transfers between devices with their start and end apart: 8 -> 9, of which waited for: 7 -> 7; matrix products, arithmetic and copies ran while one was open for 29% -> 23% of each run, Pallas kernels for 0% -> 0%
where the time goes in v1:
time: 579 us; the launch traced here: 574 us
  waiting for transfers between devices  252 us (44%)
  matrix products  87.2 us (15%)
  local copies, waits for them, and re-layouts  70.3 us (12%)
  other arithmetic  64.2 us (11%)
  starting transfers between devices  45.3 us (8%)
  blocking collectives  40.7 us (7%)
  between operations  14.3 us (2%)
    all_to_all x3, waiting for transfers between devices, all_blocks(): pieces = lax.all_to_all(pieces, axes[k], split_axis=0, concat_axis=0)  149 us
    all_to_all x3, waiting for transfers between devices, sent_to_all(): return lax.all_to_all(copies, axis, split_axis=0, concat_axis=0, tiled=True)  83.4 us
    dot_general x17, matrix products, fold_block(): jnp.einsum(forms, weights.astype(jnp.bfloat16), value_block, preferred_el...  39.1 us
    all_gather x1, blocking collectives, in_one_piece_2(): out = lax.all_gather(both, axis, axis=dim, tiled=True)  30.6 us
    reduce_sum x17, other arithmetic, fold_block(): weight_sum = weight_sum * decay + jnp.sum(weights, axis=-1)  28 us
    dot_general x8, matrix products, make_advance(): jnp.einsum('qhd,khd->hqk', query_rows, key_block, preferred_element_type=...  22.5 us
    all_to_all x3, starting transfers between devices, sent_to_all(): return lax.all_to_all(copies, axis, split_axis=0, concat_axis=0, tiled=True)  17.9 us
    all_to_all x3, starting transfers between devices, all_blocks(): pieces = lax.all_to_all(pieces, axes[k], split_axis=0, concat_axis=0)  17 us
  transfers between devices with their start and end apart: 9, of which 7 were waited for; matrix products, arithmetic and copies ran while one was open for 23% of the time, Pallas kernels for 0%

profile of v1, /device:TPU:14, one launch (start us, length us, event | category | flops | bytes accessed | tf_op | source)
XLA Modules:
  0.0 574.3 jit_solution(14416532259944610113)
XLA Ops:
  11.7 6.3 %all-to-all-start = ((bf16[64,3,16,80]{3,0,1,2:T(8,128)(2,1)}), bf16[64,3,16,80]{3,0,1,2:T(8,128)(2,1)}, u32[]{:S(2)}, u32[]{:S(2)}) async-start(bf16[64,3,16,80]{3,0,1,2:T(8,128)(2,1)} %copy.153), calls=%async_computation | async-start | bytes 1572864 | tf_op jit(solution)/shard_map/all_to_all | solution.py:115
  20.0 8.9 %all-to-all-done = bf16[64,3,16,80]{3,0,1,2:T(8,128)(2,1)} async-done(((bf16[64,3,16,80]{3,0,1,2:T(8,128)(2,1)}), bf16[64,3,16,80]{3,0,1,2:T(8,128)(2,1)}, u32[]{:S(2)}, u32[]{:S(2)}) %all-to-all-start) | async-done | bytes 491552 | tf_op jit(solution)/shard_map/all_to_all | solution.py:115
  28.9 4.3 all-to-all-start.4
  45.7 7.6 %all-to-all-start.1 = ((bf16[8,512,4,80]{1,3,2,0:T(8,128)(2,1)}), bf16[8,512,4,80]{1,3,2,0:T(8,128)(2,1)}, u32[]{:S(2)}, u32[]{:S(2)}) async-start(bf16[8,512,4,80]{1,3,2,0:T(8,128)(2,1)} %broadcast_in_dim.145), calls=%async_computation.1 | async-start | bytes 5242880 | tf_op jit(solution)/shard_map/all_to_all | solution.py:22
  53.3 61.6 %all-to-all-done.1 = bf16[8,512,4,80]{1,3,2,0:T(8,128)(2,1)} async-done(((bf16[8,512,4,80]{1,3,2,0:T(8,128)(2,1)}), bf16[8,512,4,80]{1,3,2,0:T(8,128)(2,1)}, u32[]{:S(2)}, u32[]{:S(2)}) %all-to-all-start.1) | async-done | bytes 2621472 | tf_op jit(solution)/shard_map/all_to_all | solution.py:22
  117.8 5.0 all-to-all-start.5
  126.9 76.7 %while.33 = (s32[]{:T(128)}, f32[2,512]{1,0:T(2,128)S(1)}, f32[2,512]{1,0:T(2,128)S(1)}, f32[2,512,80]{1,2,0:T(8,128)}, s32[8]{0:T(128)S(1)}, /*index=5*/s32[]{:...) while((s32[]{:T(128)}, f32[2,512]{1,0:T(2,128)S(1)}, ...), condition=%wide.region_5.6_spmd.clone, body=%wide.region_2.5_spmd.clone.sunk | while | flops 174861312 | bytes 15896233 | solution.py:147
  205.4 10.1 %all_to_all.69 = bf16[512,2,80]{2,1,0:T(2,128)(2,1)S(1)} all-to-all(bf16[512,2,80]{2,1,0:T(2,128)(2,1)} %bitcast.256), channel_id=1, replica_groups=mesh['img'=4,'seq_0'=2,'seq_1'=4,'tp'=8] {'seq_0','seq_1'}, dimensions={0} | all-to-all | bytes 327680 | tf_op jit(solution)/shard_map/all_to_all | solution.py:150
  215.6 7.1 %stack.11 = bf16[4,8,160,1024]{3,2,1,0:T(8,128)(2,1)} broadcast(bf16[8,160,1024]{2,1,0:T(8,128)(2,1)} %bitcast.38), dimensions={1,2,3} | broadcast | bytes 13107200 | tf_op jit(solution)/shard_map/stack | solution.py:49
  222.7 7.8 %all-to-all-start.6 = ((bf16[4,8,160,1024]{3,2,1,0:T(8,128)(2,1)}), bf16[4,8,160,1024]{3,2,1,0:T(8,128)(2,1)}, u32[]{:S(2)}, u32[]{:S(2)}) async-start(bf16[4,8,160,1024]{3,2,1,0:T(8,128)(2,1)} %stack.11), calls=%async_computation.6 | async-start | bytes 20971520 | tf_op jit(solution)/shard_map/all_to_all | solution.py:50
  237.2 146.2 %all-to-all-done.6 = bf16[4,8,160,1024]{3,2,1,0:T(8,128)(2,1)} async-done(((bf16[4,8,160,1024]{3,2,1,0:T(8,128)(2,1)}), bf16[4,8,160,1024]{3,2,1,0:T(8,128)(2,1)}, u32[]{:S(2)}, u32[]{:S(2)}) %all-to-all-start.6) | async-done | bytes 10485792 | tf_op jit(solution)/shard_map/all_to_all | solution.py:50
  384.6 7.1 %all-to-all-start.3 = ((bf16[8,16,5120]{2,1,0:T(8,128)(2,1)}), bf16[8,16,5120]{2,1,0:T(8,128)(2,1)S(1)}, u32[]{:S(2)}, u32[]{:S(2)}) async-start(bf16[8,16,5120]{2,1,0:T(8,128)(2,1)} %broadcast_in_dim.147), calls=%async_computation.3 | async-start | bytes 2621440 | tf_op jit(solution)/shard_map/all_to_all | solution.py:22
  392.9 4.9 fusion.55
  397.8 9.8 %copy.164 = bf16[4,8,160,1024]{3,2,0,1:T(8,128)(2,1)} copy(bf16[4,8,160,1024]{3,2,1,0:T(8,128)(2,1)} %all-to-all-done.6) | data formatting | bytes 20971520 | tf_op jit(solution)/shard_map/all_to_all | solution.py:50
  407.6 18.8 %all-to-all-done.3 = bf16[8,16,5120]{2,1,0:T(8,128)(2,1)S(1)} async-done(((bf16[8,16,5120]{2,1,0:T(8,128)(2,1)}), bf16[8,16,5120]{2,1,0:T(8,128)(2,1)S(1)}, u32[]{:S(2)}, u32[]{:S(2)}) %all-to-all-start.3) | async-done | bytes 1310752 | tf_op jit(solution)/shard_map/all_to_all | solution.py:22
  426.4 5.5 convolution_convert_fusion.1
  436.0 4.5 fusion.57
  443.6 3.7 fusion.65
  448.6 4.1 all-to-all-start.8
  454.0 7.4 %add_bitcast_fusion = f32[1,8,512,128]{3,2,1,0:T(8,128)} fusion(f32[512,512,8]{1,0,2:T(8,128)} %get-tuple-element.412, f32[8,512]{1,0:T(8,128)S(1)} %get-tuple-element.408, pred[512,512]{0,1:T(8,128)(4,1)S(1)} %iota_compare_fusion, f32[8,512]{1,0:T(8,128)S(1)} %get-tuple-element.406, bf16[1,512,1,1,128]{4,2,3,1,0:T(2,128)(2,1)S(1)} %copy-done.8), kind=kOutput, calls=%fused_computation.94 | convolution fusion | flops 547880960 | bytes 10911744 | tf_op jit(solution)/shard_map/kgcn,nkd->kgcd/dot_general | solution.py:91
  461.4 9.4 %all-to-all-done.8 = bf16[8,128,2,1,128]{4,2,1,3,0:T(2,128)(2,1)S(1)} async-done(((bf16[8,128,2,1,128]{4,2,1,3,0:T(2,128)(2,1)}), bf16[8,128,2,1,128]{4,2,1,3,0:T(2,128)(2,1)S(1)}, u32[]{:S(2)}, u32[]{:S(2)}) %all-to-all-start.8) | async-done | bytes 524320 | tf_op jit(solution)/shard_map/all_to_all | solution.py:73
  471.5 30.6 %all_gather.7 = bf16[1024,2,128]{2,0,1:T(8,128)(2,1)S(1)} all-gather(bf16[128,2,128]{2,0,1:T(8,128)(2,1)S(1)} %pad_maximum_fusion.2), channel_id=1, replica_groups=mesh['img'=4,'seq_0'=2,'seq_1'=4,'tp'=8] {'seq_0','seq_1'}, dimensions={0}, use_global_device_ids=true | all-gather | bytes 589824 | tf_op jit(solution)/shard_map/all_gather | solution.py:80
  502.8 59.9 %while.32 = (s32[]{:T(128)}, f32[1,8,512]{2,1,0:T(8,128)S(1)}, f32[1,8,512]{2,1,0:T(8,128)}, f32[1,8,512,128]{3,2,1,0:T(8,128)}, s32[8]{0:T(128)}, /*index=5*/s3...) while((s32[]{:T(128)}, f32[1,8,512]{2,1,0:T(8,128)S(1)}, ...), condition=%wide.region_14.15_spmd, body=%wide.region_11.14_spmd.sunk | while | flops 276312320 | bytes 28641332 | solution.py:224
  563.7 3.8 fusion.68
  (247 shorter events, 185.1 us)
Async XLA Ops:
  6.5 228.5 %copy-start = (bf16[1280,1280]{1,0:T(8,128)(2,1)S(1)}, bf16[1280,1280]{1,0:T(8,128)(2,1)}, u32[]{:S(2)}) copy-start(bf16[1280,1280]{1,0:T(8,128)(2,1)} %param.15) | copy-start | bytes 9830404
  11.7 17.2 %all-to-all-start = ((bf16[64,3,16,80]{3,0,1,2:T(8,128)(2,1)}), bf16[64,3,16,80]{3,0,1,2:T(8,128)(2,1)}, u32[]{:S(2)}, u32[]{:S(2)}) async-start(bf16[64,3,16,80]{3,0,1,2:T(8,128)(2,1)} %copy.153), calls=%async_computation | async-start | bytes 1572864 | tf_op jit(solution)/shard_map/all_to_all | solution.py:115
  28.9 13.9 %all-to-all-start.4 = ((bf16[2,1,160,1024]{3,2,1,0:T(8,128)(2,1)}), bf16[2,1,160,1024]{3,2,1,0:T(8,128)(2,1)}, u32[]{:S(2)}, u32[]{:S(2)}) async-start(bf16[2,1,160,1024]{3,2,1,0:T(8,128)(2,1)} %pad_maximum_fusion), calls=%async_computation.4 | async-start | bytes 1310720 | tf_op jit(solution)/shard_map/all_to_all | solution.py:50
  45.7 69.2 %all-to-all-start.1 = ((bf16[8,512,4,80]{1,3,2,0:T(8,128)(2,1)}), bf16[8,512,4,80]{1,3,2,0:T(8,128)(2,1)}, u32[]{:S(2)}, u32[]{:S(2)}) async-start(bf16[8,512,4,80]{1,3,2,0:T(8,128)(2,1)} %broadcast_in_dim.145), calls=%async_computation.1 | async-start | bytes 5242880 | tf_op jit(solution)/shard_map/all_to_all | solution.py:22
  117.8 87.6 %all-to-all-start.5 = ((bf16[4,2,160,1024]{3,2,1,0:T(8,128)(2,1)}), bf16[4,2,160,1024]{3,2,1,0:T(8,128)(2,1)}, u32[]{:S(2)}, u32[]{:S(2)}) async-start(bf16[4,2,160,1024]{3,2,1,0:T(8,128)(2,1)} %stack.10), calls=%async_computation.5 | async-start | bytes 5242880 | tf_op jit(solution)/shard_map/all_to_all | solution.py:50
  222.7 160.8 %all-to-all-start.6 = ((bf16[4,8,160,1024]{3,2,1,0:T(8,128)(2,1)}), bf16[4,8,160,1024]{3,2,1,0:T(8,128)(2,1)}, u32[]{:S(2)}, u32[]{:S(2)}) async-start(bf16[4,8,160,1024]{3,2,1,0:T(8,128)(2,1)} %stack.11), calls=%async_computation.6 | async-start | bytes 20971520 | tf_op jit(solution)/shard_map/all_to_all | solution.py:50
  230.4 213.1 %all-gather.2.cloned.1.call-start = ((), (), s32[]{:S(2)}) async-start(), calls=%async_computation.9 | async-start | bytes 4325376 | tf_op jit(solution)/shard_map/all_gather | solution.py:181
  237.2 154.6 %copy-start.7 = (bf16[1,512,2,1,128]{4,2,3,1,0:T(2,128)(2,1)S(1)}, bf16[1,512,2,1,128]{4,2,3,1,0:T(2,128)(2,1)}, u32[]{:S(2)}) copy-start(bf16[1,512,2,1,128]{4,2,3,1,0:T(2,128)(2,1)} %param.21) | copy-start | bytes 786436
  384.6 8.2 %copy-start.5 = (bf16[1,512,8,128]{3,2,1,0:T(8,128)(2,1)S(1)}, bf16[1,512,8,128]{3,2,1,0:T(8,128)(2,1)}, u32[]{:S(2)}) copy-start(bf16[1,512,8,128]{3,2,1,0:T(8,128)(2,1)} %param.20) | copy-start | bytes 3145732
  384.6 41.8 %all-to-all-start.3 = ((bf16[8,16,5120]{2,1,0:T(8,128)(2,1)}), bf16[8,16,5120]{2,1,0:T(8,128)(2,1)S(1)}, u32[]{:S(2)}, u32[]{:S(2)}) async-start(bf16[8,16,5120]{2,1,0:T(8,128)(2,1)} %broadcast_in_dim.147), calls=%async_computation.3 | async-start | bytes 2621440 | tf_op jit(solution)/shard_map/all_to_all | solution.py:22
  432.7 10.9 %all-to-all-start.7 = ((f32[8,1,128]{2,1,0:T(1,128)}), f32[8,1,128]{2,1,0:T(1,128)S(1)}, u32[]{:S(2)}, u32[]{:S(2)}) async-start(f32[8,1,128]{2,1,0:T(1,128)} %broadcast_in_dim.148), calls=%async_computation.7 | async-start | bytes 8192 | tf_op jit(solution)/shard_map/all_to_all | solution.py:22
  436.0 7.6 %copy-start.10 = (f32[1024]{0:T(1024)S(1)}, f32[1024]{0:T(1024)}, u32[]{:S(2)}) copy-start(f32[1024]{0:T(1024)} %param.18) | copy-start | bytes 12292
  447.3 6.1 %copy-start.6 = (bf16[1,512,8,128]{3,2,1,0:T(8,128)(2,1)S(1)}, bf16[1,512,8,128]{3,2,1,0:T(8,128)(2,1)}, u32[]{:S(2)}) copy-start(bf16[1,512,8,128]{3,2,1,0:T(8,128)(2,1)} %param.20) | copy-start | bytes 3145732
  447.4 6.6 %copy-start.8 = (bf16[1,512,1,1,128]{4,2,3,1,0:T(2,128)(2,1)S(1)}, bf16[1,512,1,1,128]{4,2,3,1,0:T(2,128)(2,1)}, u32[]{:S(2)}) copy-start(bf16[1,512,1,1,128]{4,2,3,1,0:T(2,128)(2,1)} %get-tuple-element.402) | copy-start | bytes 393220
  448.6 22.2 %all-to-all-start.8 = ((bf16[8,128,2,1,128]{4,2,1,3,0:T(2,128)(2,1)}), bf16[8,128,2,1,128]{4,2,1,3,0:T(2,128)(2,1)S(1)}, u32[]{:S(2)}, u32[]{:S(2)}) async-start(bf16[8,128,2,1,128]{4,2,1,3,0:T(2,128)(2,1)} %bitcast.192), calls=%async_computation.8 | async-start | bytes 1048576 | tf_op jit(solution)/shard_map/all_to_all | solution.py:73
  502.8 3.3 copy-start.3
  510.3 3.3 copy-start.3
  517.8 3.3 copy-start.3
  525.3 3.3 copy-start.3
  532.8 3.3 copy-start.3
  540.3 3.3 copy-start.3
  547.8 3.3 copy-start.3
  555.2 3.3 copy-start.3
  562.7 4.8 copy-start.1
  (17 other events, 31.6 us)
Sparse Core Ops, SparseCore 0:
  233.0 156.4 all-gather.1
